TPU v7x, 32 devices: a 4x4x1 block of a 4x4x8 slice. The times are simulated.
32 devices in a mesh: data: 1 (over z), ffn: 4 (over y), hid: 8 (over x, core).
Axes of the slice: x: 4, y: 4, z: 1, core: 2. Of those that a mesh axis runs over, the one named last changes fastest.
The devices are a block of a 4x4x8 slice.
Arguments:
- residual: bfloat16 [4096, 4096], P('data', 'hid')
- gain_mlp: float32 [4096], P('hid')
- gain_attn: float32 [4096], P('hid')
- w_gate: bfloat16 [4096, 14336], P('hid', 'ffn')
- w_up: bfloat16 [4096, 14336], P('hid', 'ffn')
- w_down: bfloat16 [14336, 4096], P('ffn', 'hid')
- w_qkv: bfloat16 [4096, 6144], P('hid', 'ffn')
Outputs:
- output 1: bfloat16 [4096, 4096], P('data', 'hid')
- output 2: bfloat16 [4096, 6144], P('data', 'ffn')
All inputs are finite; a program needn't handle non-finite values.
Results may differ from a plain program's by a relative error of at most 0.02.
Values are sent between devices in bfloat16 or wider.
A program may use at most 768 MiB of HBM per device.

v0:
```python
import jax
import jax.numpy as jnp
from jax import lax
from jax.sharding import PartitionSpec as P

NORM_EPS = 1e-6


def solution(mesh):
    hid_ways = mesh.shape['hid']

    def shard_norm(resid_shard, gain_shard, d_model):
        resid32 = resid_shard.astype(jnp.float32)
        part_sq = jnp.sum(resid32 * resid32, axis=1, keepdims=True)
        full_sq = lax.psum(part_sq, 'hid')
        scale = lax.rsqrt(full_sq / d_model + NORM_EPS)
        return (resid32 * scale * gain_shard[None, :]).astype(jnp.bfloat16)

    def device_step(residual, gain_mlp, gain_attn, w_gate, w_up, w_down, w_qkv):
        d_model = residual.shape[1] * hid_ways
        normed = shard_norm(residual, gain_mlp, d_model)
        gate_part = jnp.dot(normed, w_gate, preferred_element_type=jnp.float32).astype(jnp.bfloat16)
        up_part = jnp.dot(normed, w_up, preferred_element_type=jnp.float32).astype(jnp.bfloat16)
        gate_sum, up_sum = lax.psum((gate_part, up_part), 'hid')
        hidden_act = (jax.nn.silu(gate_sum.astype(jnp.float32)) * up_sum.astype(jnp.float32)).astype(jnp.bfloat16)
        down_part = jnp.dot(hidden_act, w_down, preferred_element_type=jnp.float32).astype(jnp.bfloat16)
        down_sum = lax.psum(down_part, 'ffn')
        residual_out = (residual.astype(jnp.float32) + down_sum.astype(jnp.float32)).astype(jnp.bfloat16)
        normed_next = shard_norm(residual_out, gain_attn, d_model)
        qkv_part = jnp.dot(normed_next, w_qkv, preferred_element_type=jnp.float32).astype(jnp.bfloat16)
        qkv_out = lax.psum(qkv_part, 'hid')
        return residual_out, qkv_out

    return jax.shard_map(
        device_step, mesh=mesh,
        in_specs=(P('data', 'hid'), P('hid'), P('hid'), P('hid', 'ffn'), P('hid', 'ffn'),
                  P('ffn', 'hid'), P('hid', 'ffn')),
        out_specs=(P('data', 'hid'), P('data', 'ffn')),
        check_vma=False)
```

profile of v0, /device:TPU:97, one launch (start us, length us, event | category | flops | bytes accessed | tf_op | source)
XLA Modules:
  0.0 964.4 jit_solution(3925018104346633451)
XLA Ops:
  7.2 0.0 copy-start
  7.2 0.1 all-reduce.9.cloned.1.call-start
  7.3 3.2 fusion.10
  10.5 24.0 %psum.42 = f32[4096,1]{0,1:T(1,128)S(1)} all-reduce(f32[4096,1]{0,1:T(1,128)S(1)} %bitcast.9), channel_id=1, replica_groups=mesh['data'=1,'ffn'=4,'hid'=8] {'hid'}, use_global_device_ids=true, to_apply=%region_1.0 | all-reduce | flops 4096 | bytes 32768 | tf_op jit(solution)/shard_map/psum | solution.py:15
  34.5 0.0 copy-start.1
  34.5 0.0 copy-start.2
  34.5 22.9 %convolution_convert_fusion = bf16[4096,3584]{1,0:T(8,128)(2,1)} fusion(bf16[512,3584]{1,0:T(8,128)(2,1)} %param.11, bf16[4096,512]{1,0:T(8,128)(2,1)} %param.7, f32[512]{0:T(512)} %param.8, f32[4096]{0:T(1024)S(1)} %bitcast.10), kind=kOutput, calls=%fused_computation.7 | convolution fusion | flops 15055454208 | bytes 37242880 | tf_op jit(solution)/shard_map/dot_general | solution.py:23
  57.4 0.0 copy-done.1
  57.4 0.0 copy-done.2
  57.4 21.1 %convolution_convert_fusion.1 = bf16[4096,3584]{1,0:T(8,128)(2,1)} fusion(bf16[512,3584]{1,0:T(8,128)(2,1)} %param.10, bf16[4096,512]{1,0:T(8,128)(2,1)S(1)} %copy-done.1, f32[512]{0:T(512)S(1)} %copy-done.2, f32[4096]{0:T(1024)S(1)} %bitcast.11), kind=kOutput, calls=%fused_computation.8 | convolution fusion | flops 15055454208 | bytes 37242880 | tf_op jit(solution)/shard_map/dot_general | solution.py:22
  78.5 0.1 all-reduce.9.cloned.1.call-update
  78.6 0.2 all-reduce.5.cloned.1.call-start
  78.8 574.3 %all-reduce.9.cloned.1.call-done = (bf16[4096,3584]{1,0:T(8,128)(2,1)}, bf16[4096,3584]{1,0:T(8,128)(2,1)}) async-done(((bf16[4096,3584]{1,0:T(8,128)(2,1)}, bf16[4096,3584]{1,0:T(8,128)(2,1)}), (bf16[4096,3584]{1,0:T(8,128)(2,1)}, bf16[4096,3584]{1,0:T(8,128)(2,1)})) %all-reduce.9.cloned.1.call-update) | async-done | bytes 58720272 | tf_op jit(solution)/shard_map/psum | solution.py:24
  653.1 26.2 %fusion.14 = bf16[4096,512]{1,0:T(8,128)(2,1)} fusion(bf16[3584,512]{1,0:T(8,128)(2,1)} %param.12, bf16[4096,3584]{1,0:T(8,128)(2,1)} %get-tuple-element.2, bf16[4096,3584]{1,0:T(8,128)(2,1)} %get-tuple-element.3), kind=kOutput, calls=%fused_computation.23 | convolution fusion | flops 15151923200 | bytes 66584576 | tf_op jit(solution)/shard_map/dot_general | solution.py:26
  679.3 0.0 copy-start.3
  679.3 0.1 all-reduce.5.cloned.1.call-update
  679.3 0.1 all-reduce.7.cloned.1.call-start
  679.4 87.5 %all-reduce.5.cloned.1.call-done = bf16[4096,512]{1,0:T(8,128)(2,1)} async-done(((bf16[4096,512]{1,0:T(8,128)(2,1)}), bf16[4096,512]{1,0:T(8,128)(2,1)}) %all-reduce.5.cloned.1.call-update) | async-done | bytes 4194320 | tf_op jit(solution)/shard_map/psum | solution.py:27
  766.9 7.0 fusion.7
  773.9 22.7 %psum.46 = f32[4096,1]{0,1:T(1,128)S(1)} all-reduce(f32[4096,1]{0,1:T(1,128)S(1)} %bitcast.8), channel_id=1, replica_groups=mesh['data'=1,'ffn'=4,'hid'=8] {'hid'}, use_global_device_ids=true, to_apply=%region_6.7 | all-reduce | flops 4096 | bytes 32768 | tf_op jit(solution)/shard_map/psum | solution.py:15
  796.6 0.0 copy-done
  796.6 0.0 copy-done.3
  796.6 12.1 %convolution_convert_fusion.2 = bf16[4096,1536]{1,0:T(8,128)(2,1)} fusion(bf16[512,1536]{1,0:T(8,128)(2,1)S(1)} %copy-done, bf16[4096,512]{1,0:T(8,128)(2,1)} %get-tuple-element.6, f32[512]{0:T(512)S(1)} %copy-done.3, f32[4096]{0:T(1024)S(1)} %bitcast.12), kind=kOutput, calls=%fused_computation.10 | convolution fusion | flops 6457131008 | bytes 18368512 | tf_op jit(solution)/shard_map/dot_general | solution.py:30
  808.7 0.1 all-reduce.7.cloned.1.call-update
  808.7 138.7 %all-reduce.7.cloned.1.call-done = bf16[4096,1536]{1,0:T(8,128)(2,1)} async-done(((bf16[4096,1536]{1,0:T(8,128)(2,1)}), bf16[4096,1536]{1,0:T(8,128)(2,1)}) %all-reduce.7.cloned.1.call-update) | async-done | bytes 12582928 | tf_op jit(solution)/shard_map/psum | solution.py:31
  947.5 10.5 %copy.13 = bf16[4096,1536]{1,0:T(8,128)(2,1)} copy(bf16[4096,1536]{1,0:T(8,128)(2,1)} %all-reduce.7.cloned.1.call-done) | data formatting | bytes 25165824
  (2 shorter events, 0.1 us)
Async XLA Ops:
  7.2 789.4 %copy-start = (bf16[512,1536]{1,0:T(8,128)(2,1)S(1)}, bf16[512,1536]{1,0:T(8,128)(2,1)}, u32[]{:S(2)}) copy-start(bf16[512,1536]{1,0:T(8,128)(2,1)} %param.13) | copy-start | bytes 4718596
  7.2 645.9 %all-reduce.9.cloned.1.call-start = ((), (), s32[]{:S(2)}) async-start(), calls=%async_computation.2 | async-start | bytes 117440512 | tf_op jit(solution)/shard_map/psum | solution.py:24
  34.5 22.9 %copy-start.1 = (bf16[4096,512]{1,0:T(8,128)(2,1)S(1)}, bf16[4096,512]{1,0:T(8,128)(2,1)}, u32[]{:S(2)}) copy-start(bf16[4096,512]{1,0:T(8,128)(2,1)} %param.7) | copy-start | bytes 12582916
  34.5 22.9 %copy-start.2 = (f32[512]{0:T(512)S(1)}, f32[512]{0:T(512)}, u32[]{:S(2)}) copy-start(f32[512]{0:T(512)} %param.8) | copy-start | bytes 6148
  78.6 688.3 %all-reduce.5.cloned.1.call-start = ((), (), s32[]{:S(2)}) async-start(), calls=%async_computation | async-start | bytes 8388608 | tf_op jit(solution)/shard_map/psum | solution.py:27
  679.3 117.3 %copy-start.3 = (f32[512]{0:T(512)S(1)}, f32[512]{0:T(512)}, u32[]{:S(2)}) copy-start(f32[512]{0:T(512)} %param.9) | copy-start | bytes 6148
  679.3 268.1 %all-reduce.7.cloned.1.call-start = ((), (), s32[]{:S(2)}) async-start(), calls=%async_computation.1 | async-start | bytes 25165824 | tf_op jit(solution)/shard_map/psum | solution.py:31
Sparse Core Ops, SparseCore 0:
  78.7 574.3 all-reduce.8
  679.5 87.3 all-reduce.4
  808.8 138.5 all-reduce.6
where the time goes:
time: 965 us; the launch traced here: 964 us
  waiting for transfers between devices  801 us (83%)
  matrix products  82.2 us (9%)
  blocking collectives  46.7 us (5%)
  between operations  13.8 us (1%)
  local copies, waits for them, and re-layouts  10.5 us (1%)
  other arithmetic  10.2 us (1%)
    psum x1, waiting for transfers between devices, device_step(): gate_sum, up_sum = lax.psum((gate_part, up_part), 'hid')  574 us
    psum x1, waiting for transfers between devices, device_step(): qkv_out = lax.psum(qkv_part, 'hid')  139 us
    psum x1, waiting for transfers between devices, device_step(): down_sum = lax.psum(down_part, 'ffn')  87.5 us
    psum x2, blocking collectives, shard_norm(): full_sq = lax.psum(part_sq, 'hid')  46.7 us
    dot_general x1, matrix products, device_step(): jnp.dot(hidden_act, w_down, preferred_element_type=jnp.float32)  26.2 us
    dot_general x1, matrix products, device_step(): jnp.dot(normed, w_up, preferred_element_type=jnp.float32)  22.9 us
    dot_general x1, matrix products, device_step(): jnp.dot(normed, w_gate, preferred_element_type=jnp.float32)  21.1 us
  transfers between devices with their start and end apart: 3, of which 3 were waited for; matrix products, arithmetic and copies ran while one was open for 0% of the time, Pallas kernels for 0%

commit v1 on v0

v1 whole, which is shorter than its diff:
```python
import functools

import jax
import jax.numpy as jnp
from jax import lax
from jax.experimental import pallas as pl
from jax.experimental.pallas import tpu as pltpu
from jax.sharding import PartitionSpec as P

NORM_EPS = 1e-6
MESH = pl.DeviceIdType.MESH
N_CHUNK = 4
Q_CHUNK = 2


class Ring:
    def __init__(self, me, dev, slot, send, recv):
        self.me, self.dev, self.slot, self.send, self.recv = me, dev, slot, send, recv
        self.right, self.left, self.far = (lax.rem(me + d, 4) for d in (1, 3, 2))

    def copy(self, k, n, owner, half, target, src=None):
        dst = self.slot(k, owner, half)
        return pltpu.make_async_remote_copy(
            src_ref=dst if src is None else src, dst_ref=dst,
            send_sem=self.send.at[k, n], recv_sem=self.recv.at[k, n],
            device_id=self.dev(target), device_id_type=MESH)

    def start_own(self, k, src=None):
        for n, half, target in ((0, 0, self.right), (3, 1, self.left), (1, 1, self.right), (4, 0, self.left)):
            self.copy(k, n, self.me, half, target, None if src is None else src(k, half)).start()

    def forward(self, k):
        self.copy(k, 0, self.left, 0, self.right).wait_recv()
        self.copy(k, 2, self.left, 0, self.right).start()
        self.copy(k, 3, self.right, 1, self.left).wait_recv()
        self.copy(k, 5, self.right, 1, self.left).start()

    def wait_left(self, k):
        self.copy(k, 1, self.left, 1, self.right).wait_recv()

    def wait_right(self, k):
        self.copy(k, 4, self.right, 0, self.left).wait_recv()

    def wait_far(self, k):
        self.copy(k, 2, self.far, 0, self.right).wait_recv()
        self.copy(k, 5, self.far, 1, self.left).wait_recv()

    def finish(self, k):
        self.wait_left(k)
        self.wait_right(k)
        self.wait_far(k)

    def drain(self, k):
        for n, owner, half, target in ((0, self.me, 0, self.right), (1, self.me, 1, self.right),
                                       (2, self.left, 0, self.right), (3, self.me, 1, self.left),
                                       (4, self.me, 0, self.left), (5, self.right, 1, self.left)):
            self.copy(k, n, owner, half, target).wait_send()


def kernel(d_model, x, gains, w_gate, w_up, w_down, w_qkv,
           x2_out, qkv_out, n_all, wq_all,
           xg, n_own, n_in, w_in, stage, act, wd_in, part, got, q_stage, gain_buf,
           loc, one_s, one_r, gain_s, gain_r, xd_s, xd_r, wx_s, wx_r, wd_s, wd_r, wq_s, wq_r, wqd_s, wqd_r,
           rs_s, rs_r, qy_s, qy_r, qd_s, qd_r,
           xr_s, xr_r, nr_s, nr_r, ar_s, ar_r, wr_s, wr_r, x2r_s, x2r_r, or_s, or_r, qr_s, qr_r):
    hid, row = lax.axis_index('hid'), lax.axis_index('ffn')
    chip, core = lax.div(hid, 2), lax.rem(hid, 2)
    mate = hid + 1 - 2 * core
    right, left, far = (lax.rem(chip + d, 4) for d in (1, 3, 2))
    tokens, width = x.shape
    half_t, block = tokens // 2, tokens // 8
    sub = block // 2
    ff = w_gate.shape[1] // 4
    qb = w_qkv.shape[1] // 4
    nc, qc = block // N_CHUNK, block // Q_CHUNK

    def dev_x(c):
        return {'hid': 2 * c + core, 'ffn': row}

    def dev_y(r):
        return {'hid': hid, 'ffn': r}

    mate_dev = {'hid': mate, 'ffn': row}

    def remote(src, dst, s, r, dev):
        return pltpu.make_async_remote_copy(src_ref=src, dst_ref=dst, send_sem=s, recv_sem=r,
                                            device_id=dev, device_id_type=MESH)

    def local(src, dst, n):
        return pltpu.make_async_copy(src, dst, loc.at[n])

    def rows_of(c, r):
        return c * half_t + r * block

    def ds(start, size):
        return pl.ds(pl.multiple_of(start, size), size)

    barrier = pltpu.get_barrier_semaphore()
    for d in range(1, 8):
        pl.semaphore_signal(barrier, inc=1, device_id={'hid': lax.rem(hid + d, 8), 'ffn': row}, device_id_type=MESH)
    for d in range(1, 4):
        pl.semaphore_signal(barrier, inc=1, device_id=dev_y(lax.rem(row + d, 4)), device_id_type=MESH)
    pl.semaphore_wait(barrier, 10)

    def x_chunk(k, c):
        return x.at[ds(rows_of(c, row) + k * nc, nc), :]

    def xd(k, h, c):
        return remote(x_chunk(k, c), xg.at[h, k * nc:(k + 1) * nc, :], xd_s.at[k], xd_r.at[k], mate_dev)

    x_own = [local(x_chunk(k, core), xg.at[hid, k * nc:(k + 1) * nc, :], k) for k in range(N_CHUNK)]
    for k in range(N_CHUNK):
        xd(k, hid, 1 - core).start()
        x_own[k].start()

    def gain_copy(d):
        to = lax.rem(hid + d, 8)
        return remote(gains, gain_buf.at[hid], gain_s.at[d - 1], gain_r.at[d - 1], {'hid': to, 'ffn': row})

    def gain_got(d):
        src = lax.rem(hid + 8 - d, 8)
        return remote(gains, gain_buf.at[src], gain_s.at[d - 1], gain_r.at[d - 1], {'hid': src, 'ffn': row})

    for d in range(1, 8):
        gain_copy(d).start()
    gain_own = local(gains, gain_buf.at[hid], 4)
    gain_own.start()

    x_ring = Ring(chip, dev_x, lambda k, c, h: xg.at[2 * c + h, k * nc:(k + 1) * nc, :], xr_s, xr_r)
    for k in range(N_CHUNK):
        x_own[k].wait()
        xd(k, mate, core).wait_recv()
        x_ring.start_own(k)

    mats = (w_gate, w_up)

    def cols(m, c):
        return mats[m].at[:, ds(c * ff, ff)]

    def w_rows(m, h):
        return w_in.at[ds(h * width, width), m * ff:(m + 1) * ff]

    w_own = [local(cols(m, chip), w_rows(m, hid), 5 + m) for m in range(2)]
    wd_own = local(w_down, wd_in.at[core], 7)
    for c in (*w_own, wd_own):
        c.start()
    wd_mate = remote(w_down, wd_in.at[core], one_s.at[0], one_r.at[0], mate_dev)
    wd_mate.start()

    def w_mate(n, m, h):
        return remote(w_rows(m, h), w_rows(m, h), wd_s.at[n, m], wd_r.at[n, m], mate_dev)

    for m in range(2):
        remote(cols(m, chip), w_rows(m, hid), wd_s.at[0, m], wd_r.at[0, m], mate_dev).start()

    for k in range(N_CHUNK):
        x_ring.forward(k)

    hw = width // 2

    def far_half(m, side, c):
        return mats[m].at[side * hw:(side + 1) * hw, ds(c * ff, ff)]

    def half_rows(m, h, side):
        return w_in.at[ds(h * width + side * hw, hw), m * ff:(m + 1) * ff]

    for m in range(2):
        remote(far_half(m, 0, far), stage.at[0, m], wx_s.at[0, m], wx_r.at[0, m], dev_x(right)).start()
        remote(far_half(m, 1, far), stage.at[1, m], wx_s.at[1, m], wx_r.at[1, m], dev_x(left)).start()
    for m in range(2):
        remote(cols(m, right), w_rows(m, hid), wx_s.at[2, m], wx_r.at[2, m], dev_x(right)).start()
        remote(cols(m, left), w_rows(m, hid), wx_s.at[3, m], wx_r.at[3, m], dev_x(left)).start()

    wq_in = local(w_qkv.at[:, ds(chip * qb, qb)], q_stage.at[0:width, 0:qb], 8)
    wq_in.start()
    for n, c in enumerate((right, left, far)):
        remote(w_qkv.at[:, ds(c * qb, qb)], wq_all.at[row, core, chip], wq_s.at[n], wq_r.at[n], dev_x(c)).start()

    n_ring = Ring(row, dev_y, lambda k, r, h: n_all.at[r, k * nc + h * (nc // 2):k * nc + (h + 1) * (nc // 2), :],
                  nr_s, nr_r)

    def n_src(k, h):
        return n_own.at[k * nc + h * (nc // 2):k * nc + (h + 1) * (nc // 2), :]

    def norm(start, count, which):
        tile = min(16, count)

        def body(t, carry):
            rows = ds(start + t * tile, tile)
            total = jnp.zeros((tile, 1), jnp.float32)
            for h in range(8):
                piece = xg[h, rows, :].astype(jnp.float32)
                total += jnp.sum(piece * piece, axis=1, keepdims=True)
            scale = lax.rsqrt(total / d_model + NORM_EPS)
            for h in range(8):
                piece = xg[h, rows, :].astype(jnp.float32)
                n_own[rows, h * width:(h + 1) * width] = (
                    piece * scale * gain_buf[h, which:which + 1, :]).astype(n_own.dtype)
            return carry

        lax.fori_loop(0, count // tile, body, 0)

    gain_own.wait()
    for d in range(1, 8):
        gain_got(d).wait_recv()
    n_keep = [local(n_own.at[k * nc:(k + 1) * nc, :], n_all.at[row, k * nc:(k + 1) * nc, :], 9 + k)
              for k in range(N_CHUNK)]
    for k in range(N_CHUNK):
        x_ring.finish(k)
        norm(k * nc, nc, 0)
        n_ring.start_own(k, n_src)
        n_keep[k].start()

    wq_in.wait()
    wq_keep = local(q_stage.at[0:width, 0:qb], wq_all.at[row, core, chip], 8)
    wq_keep.start()

    n_ring.forward(0)
    for m in range(2):
        remote(stage.at[0, m], stage.at[0, m], wx_s.at[0, m], wx_r.at[0, m], dev_x(right)).wait_recv()
        remote(stage.at[0, m], half_rows(m, 2 * left + core, 0), wx_s.at[4, m], wx_r.at[4, m], dev_x(right)).start()
        remote(stage.at[1, m], stage.at[1, m], wx_s.at[1, m], wx_r.at[1, m], dev_x(left)).wait_recv()
        remote(stage.at[1, m], half_rows(m, 2 * right + core, 1), wx_s.at[5, m], wx_r.at[5, m], dev_x(left)).start()
    n_ring.forward(1)
    n_ring.forward(2)
    for m in range(2):
        remote(w_rows(m, hid), w_rows(m, 2 * left + core), wx_s.at[2, m], wx_r.at[2, m], dev_x(right)).wait_recv()
        w_mate(1, m, 2 * left + core).start()
        remote(w_rows(m, hid), w_rows(m, 2 * right + core), wx_s.at[3, m], wx_r.at[3, m], dev_x(left)).wait_recv()
        w_mate(2, m, 2 * right + core).start()
    n_ring.forward(3)
    for m in range(2):
        h = 2 * far + core
        remote(stage.at[0, m], half_rows(m, h, 0), wx_s.at[4, m], wx_r.at[4, m], dev_x(right)).wait_recv()
        remote(stage.at[1, m], half_rows(m, h, 1), wx_s.at[5, m], wx_r.at[5, m], dev_x(left)).wait_recv()
        w_mate(3, m, h).start()
    wq_keep.wait()
    for n, c in enumerate((left, right, far)):
        remote(w_qkv.at[:, ds(c * qb, qb)], wq_all.at[row, core, c], wq_s.at[n], wq_r.at[n], dev_x(c)).wait_recv()
    wq_ring = Ring(row, dev_y, lambda k, r, h: wq_all.at[r, core, 2 * h:2 * h + 2], wr_s, wr_r)
    for c in w_own:
        c.wait()
    for m in range(2):
        for n, c in enumerate((chip, left, right, far)):
            w_mate(n, m, 2 * c + 1 - core).wait_recv()
    wd_own.wait()
    remote(w_down, wd_in.at[1 - core], one_s.at[0], one_r.at[0], mate_dev).wait_recv()
    for k in range(N_CHUNK):
        n_keep[k].wait()
        x_ring.drain(k)

    a_ring = Ring(chip, dev_x, lambda s, c, h: act.at[s, h * (sub // 2):(h + 1) * (sub // 2), ds(c * ff, ff)],
                  ar_s, ar_r)

    def n_load(s):
        r = lax.rem(row + lax.div(s, 2) + 1, 4)
        return local(n_all.at[r, ds(lax.rem(s, 2) * sub, sub), :], n_in, 13)

    def part_copy(s, back):
        d = lax.div(s, 2) + 1
        to = lax.rem(row + d, 4)
        return remote(part.at[s], got.at[s], rs_s.at[s], rs_r.at[s], dev_y(to))

    for k in range(N_CHUNK):
        n_ring.wait_right(k)
    n_load(0).start()

    def step(s, carry):
        @pl.when(s < 8)
        def _():
            n_load(s).wait()
            gate = jnp.dot(n_in[...], w_in[:, 0:ff], preferred_element_type=jnp.float32).astype(jnp.bfloat16)
            up = jnp.dot(n_in[...], w_in[:, ff:2 * ff], preferred_element_type=jnp.float32).astype(jnp.bfloat16)
            act[s, :, ds(chip * ff, ff)] = (
                jax.nn.silu(gate.astype(jnp.float32)) * up.astype(jnp.float32)).astype(act.dtype)
            a_ring.start_own(s)

        @pl.when((s >= 1) & (s < 9))
        def _():
            a_ring.forward(s - 1)

        @pl.when(s == 1)
        def _():
            for k in range(N_CHUNK):
                n_ring.wait_far(k)

        @pl.when(s == 3)
        def _():
            for k in range(N_CHUNK):
                n_ring.wait_left(k)
            wq_ring.start_own(0)

        @pl.when(s == 6)
        def _():
            wq_ring.forward(0)

        @pl.when(s < 7)
        def _():
            n_load(s + 1).start()

        @pl.when(s >= 2)
        def _():
            b = s - 2
            a_ring.finish(b)
            for c in range(2):
                part[b, c] = jnp.dot(act[b], wd_in[c], preferred_element_type=jnp.float32).astype(part.dtype)

            @pl.when(b < 6)
            def _():
                part_copy(b, 0).start()

        return carry

    lax.fori_loop(0, 10, step, 0)

    wq_ring.finish(0)
    for r in range(4):
        remote(wq_all.at[r, core], wq_all.at[r, core], wqd_s.at[r], wqd_r.at[r], mate_dev).start()

    for s in range(6):
        part_copy(s, 0).wait_recv()
    for k in range(N_CHUNK):
        n_ring.drain(k)
    tile = min(16, sub)
    for s in range(2):
        def add(t, carry):
            rows = ds(t * tile, tile)
            out_rows = ds(s * sub + t * tile, tile)
            for c in range(2):
                down = part[6 + s, c, rows, :].astype(jnp.float32)
                for q in range(3):
                    down += got[2 * q + s, c, rows, :].astype(jnp.float32)
                old = xg[2 * chip + c, out_rows, :].astype(jnp.float32)
                xg[2 * chip + c, out_rows, :] = (
                    old + down.astype(jnp.bfloat16).astype(jnp.float32)).astype(xg.dtype)
            return carry

        lax.fori_loop(0, sub // tile, add, 0)

    x2_ring = Ring(chip, dev_x, lambda k, c, h: xg.at[2 * c + h, k * qc:(k + 1) * qc, :], x2r_s, x2r_r)
    for k in range(Q_CHUNK):
        x2_ring.start_own(k)

    def x2_rows(c, r):
        return x2_out.at[ds(rows_of(c, r), block), :]

    x2_keep = local(xg.at[hid], x2_rows(core, row), 0)
    x2_keep.start()
    x2_mate = remote(xg.at[mate], x2_rows(core, row), one_s.at[1], one_r.at[1], mate_dev)
    x2_mate.start()

    for r in range(4):
        remote(wq_all.at[r, 1 - core], wq_all.at[r, 1 - core], wqd_s.at[r], wqd_r.at[r], mate_dev).wait_recv()

    def wq_load(r, c, i):
        return local(wq_all.at[r, c, i], w_in.at[(2 * i + c) * width:(2 * i + c + 1) * width, r * qb:(r + 1) * qb],
                     16 + r * 8 + c * 4 + i)

    wq_loads = [wq_load(r, c, i) for r in range(4) for c in range(2) for i in range(4)]
    for m in range(2):
        for n in range(4):
            w_mate(n, m, hid).wait_send()
    for c in wq_loads:
        c.start()

    for k in range(Q_CHUNK):
        x2_ring.forward(k)
    x2_keep.wait()
    remote(xg.at[mate], x2_rows(1 - core, row), one_s.at[1], one_r.at[1], mate_dev).wait_recv()
    out_ring = Ring(row, dev_y, lambda k, r, h: x2_rows(h, r), or_s, or_r)
    out_ring.start_own(0)
    for c in wq_loads:
        c.wait()

    def q_rows(r, start, count):
        return ds(rows_of(core, r) + start, count)

    def qy(k, n, r):
        return remote(q_stage.at[k * qc:(k + 1) * qc, ds(r * qb, qb)],
                      qkv_out.at[q_rows(row, k * qc, qc), ds(chip * qb, qb)],
                      qy_s.at[k, n], qy_r.at[k, n], dev_y(r))

    def qy_got(k, n, r):
        return remote(q_stage.at[k * qc:(k + 1) * qc, ds(r * qb, qb)],
                      qkv_out.at[q_rows(r, k * qc, qc), ds(chip * qb, qb)],
                      qy_s.at[k, n], qy_r.at[k, n], dev_y(r))

    q_keep = [local(q_stage.at[k * qc:(k + 1) * qc, ds(row * qb, qb)],
                    qkv_out.at[q_rows(row, k * qc, qc), ds(chip * qb, qb)], 1 + k) for k in range(Q_CHUNK)]
    for k in range(Q_CHUNK):
        x2_ring.finish(k)
        norm(k * qc, qc, 1)
        q_stage[k * qc:(k + 1) * qc, :] = jnp.dot(
            n_own[k * qc:(k + 1) * qc, :], w_in[:, 0:4 * qb], preferred_element_type=jnp.float32).astype(q_stage.dtype)
        for n in range(3):
            qy(k, n, lax.rem(row + n + 1, 4)).start()
        q_keep[k].start()
    out_ring.forward(0)

    q_ring = Ring(chip, dev_x,
                  lambda n, c, h: qkv_out.at[ds(rows_of(core, lax.rem(row + 4 - n, 4)) + h * sub, sub), ds(c * qb, qb)],
                  qr_s, qr_r)

    def q_mate(n, c):
        rows = ds(rows_of(c, lax.rem(row + 4 - n, 4)), block)
        return remote(qkv_out.at[rows, :], qkv_out.at[rows, :], qd_s.at[n], qd_r.at[n], mate_dev)

    for c in q_keep:
        c.wait()
    q_ring.start_own(0)
    for n in range(1, 4):
        for k in range(Q_CHUNK):
            qy_got(k, n - 1, lax.rem(row + 4 - n, 4)).wait_recv()
        q_ring.start_own(n)
        q_ring.forward(n - 1)
        if n >= 2:
            q_ring.finish(n - 2)
            q_mate(n - 2, core).start()
    q_ring.forward(3)
    for n in (2, 3):
        q_ring.finish(n)
        q_mate(n, core).start()
    out_ring.finish(0)

    for n in range(4):
        q_mate(n, 1 - core).wait_recv()
    for d in range(1, 8):
        gain_copy(d).wait_send()
    for k in range(N_CHUNK):
        xd(k, hid, 1 - core).wait_send()
    wd_mate.wait_send()
    x2_mate.wait_send()
    for m in range(2):
        for n in range(6):
            remote(stage.at[0, m] if n in (0, 1, 4, 5) else w_rows(m, hid),
                   stage.at[0, m] if n in (0, 1, 4, 5) else w_rows(m, hid),
                   wx_s.at[n, m], wx_r.at[n, m], dev_x(right)).wait_send()
    for n in range(3):
        remote(wq_all.at[row, core, chip], wq_all.at[row, core, chip], wq_s.at[n], wq_r.at[n],
               dev_x(right)).wait_send()
    for r in range(4):
        remote(wq_all.at[r, core], wq_all.at[r, core], wqd_s.at[r], wqd_r.at[r], mate_dev).wait_send()
    for s in range(6):
        part_copy(s, 0).wait_send()
    for k in range(Q_CHUNK):
        for n in range(3):
            qy(k, n, lax.rem(row + n + 1, 4)).wait_send()
        x2_ring.drain(k)
    for n in range(4):
        q_mate(n, core).wait_send()
        q_ring.drain(n)

    def drain_act(s, carry):
        a_ring.drain(s)
        return carry

    lax.fori_loop(0, 8, drain_act, 0)
    wq_ring.drain(0)
    out_ring.drain(0)


def solution(mesh):
    hid_ways, ffn_ways = mesh.shape['hid'], mesh.shape['ffn']
    assert hid_ways == 8 and ffn_ways == 4

    def device_step(residual, gain_mlp, gain_attn, w_gate, w_up, w_down, w_qkv):
        tokens, width = residual.shape
        d_model = width * hid_ways
        block, sub = tokens // 8, tokens // 16
        ff, qb = w_gate.shape[1] // 4, w_qkv.shape[1] // 4
        gains = jnp.stack([gain_mlp, gain_attn])
        dtype = residual.dtype
        any_spec = pl.BlockSpec(memory_space=pl.ANY)
        dma = pltpu.SemaphoreType.DMA
        outs = pl.pallas_call(
            functools.partial(kernel, d_model),
            out_shape=(jax.ShapeDtypeStruct((tokens, width), dtype),
                       jax.ShapeDtypeStruct((tokens, w_qkv.shape[1]), dtype),
                       jax.ShapeDtypeStruct((4, block, d_model), dtype),
                       jax.ShapeDtypeStruct((4, 2, 4, width, qb), dtype)),
            in_specs=[any_spec] * 6,
            out_specs=(any_spec,) * 4,
            scratch_shapes=[
                pltpu.VMEM((8, block, width), dtype),
                pltpu.VMEM((block, d_model), dtype),
                pltpu.VMEM((sub, d_model), dtype),
                pltpu.VMEM((d_model, 2 * ff), dtype),
                pltpu.VMEM((2, 2, width // 2, ff), dtype),
                pltpu.VMEM((8, sub, 4 * ff), dtype),
                pltpu.VMEM((2, 4 * ff, width), dtype),
                pltpu.VMEM((8, 2, sub, width), dtype),
                pltpu.VMEM((6, 2, sub, width), dtype),
                pltpu.VMEM((max(block, width), 4 * qb), dtype),
                pltpu.VMEM((8, 2, width), jnp.float32),
                dma((48,)), dma((2,)), dma((2,)), dma((7,)), dma((7,)),
                dma((N_CHUNK,)), dma((N_CHUNK,)), dma((6, 2)), dma((6, 2)), dma((4, 2)), dma((4, 2)),
                dma((3,)), dma((3,)), dma((4,)), dma((4,)), dma((6,)), dma((6,)),
                dma((Q_CHUNK, 3)), dma((Q_CHUNK, 3)), dma((4,)), dma((4,)),
                dma((N_CHUNK, 6)), dma((N_CHUNK, 6)), dma((N_CHUNK, 6)), dma((N_CHUNK, 6)),
                dma((8, 6)), dma((8, 6)), dma((1, 6)), dma((1, 6)), dma((Q_CHUNK, 6)), dma((Q_CHUNK, 6)),
                dma((1, 6)), dma((1, 6)), dma((4, 6)), dma((4, 6)),
            ],
            compiler_params=pltpu.CompilerParams(
                collective_id=0, has_side_effects=True, vmem_limit_bytes=67043328),
            name='layer',
        )(residual, gains, w_gate, w_up, w_down, w_qkv)
        return outs[0], outs[1]

    return jax.shard_map(
        device_step, mesh=mesh,
        in_specs=(P('data', 'hid'), P('hid'), P('hid'), P('hid', 'ffn'), P('hid', 'ffn'),
                  P('ffn', 'hid'), P('hid', 'ffn')),
        out_specs=(P('data', 'hid'), P('data', 'ffn')),
        check_vma=False)
```

time: 965 us -> 412 us (0.43)
  waiting for transfers between devices: 801 us -> 0 us
  Pallas kernels: 0 us -> 395 us
  matrix products: 82.2 us -> 0 us
  blocking collectives: 46.7 us -> 0 us
  between operations: 13.8 us -> 0.64 us
    psum x3 -> x0, waiting for transfers between devices: 800 us -> none  [the longest x1 574 us: device_step(): gate_sum, up_sum = lax.psum((gate_part, up_part), 'hid')]
    pallas_call x0 -> x1, Pallas kernels: none -> 395 us  [device_step(): pl.pallas_call(functools.partial(kernel, d_model), out_shape=(jax.ShapeDt...]
    dot_general x4 -> x0, matrix products: 82.2 us -> none  [the longest x1 26.2 us: device_step(): jnp.dot(hidden_act, w_down, preferred_element_type=jnp.float32)]
    psum x2 -> x0, blocking collectives: 46.7 us -> none  [shard_norm(): full_sq = lax.psum(part_sq, 'hid')]
    reduce_sum x2 -> x0, other arithmetic: 10.2 us -> none  [shard_norm(): part_sq = jnp.sum(resid32 * resid32, axis=1, keepdims=True)]
  transfers between devices with their start and end apart: 3 -> 0, of which waited for: 3 -> 0; matrix products, arithmetic and copies ran while one was open for 0% -> 0% of each run, Pallas kernels for 0% -> 0%
where the time goes in v1:
time: 412 us
  Pallas kernels  395 us (96%)
  local copies, waits for them, and re-layouts  14.9 us (4%)
    pallas_call x1, Pallas kernels, device_step(): pl.pallas_call(functools.partial(kernel, d_model), out_shape=(jax.ShapeDt...  395 us
    unnamed x2, local copies, waits for them, and re-layouts  14.9 us

profile of v1, /device:TPU:97, one launch (start us, length us, event | category | flops | bytes accessed | tf_op | source)
XLA Modules:
  0.0 411.8 jit_solution(507915127352560003)
XLA Ops:
  0.6 1.3 pad_maximum_fusion.gains
  1.9 395.0 %layer.1 = (bf16[4096,512]{1,0:T(8,128)(2,1)}, bf16[4096,1536]{1,0:T(8,128)(2,1)}, bf16[4,512,4096]{2,1,0:T(8,128)(2,1)}, bf16[4,2,4,512,384]{4,3,2,1,0:T(8,128)(2,1)}) custom-call(bf16[4096,512]{1,0:T(8,128)(2,1)} %x.1, f32[2,512]{1,0:T(2,128)} %pad_maximum_fusion.gains, bf16[512,3584]{1,0:T(8,128)(2,1)} %w_gate.1, bf16[512,3584]{1,0:T(8,128)(2,1)} %w_up.1, ...), custom_call_target="tpu_custom_call" | custom-call | tf_op jit(solution)/shard_map/layer/pallas_call | solution.py:475
  396.9 4.5 %copy.11 = bf16[4096,512]{1,0:T(8,128)(2,1)} copy(bf16[4096,512]{1,0:T(8,128)(2,1)} %get-tuple-element.8) | data formatting | bytes 8388608
  401.4 10.5 %copy.12 = bf16[4096,1536]{1,0:T(8,128)(2,1)} copy(bf16[4096,1536]{1,0:T(8,128)(2,1)} %get-tuple-element.9) | data formatting | bytes 25165824

commit v2 on v1

--- a/solution.py
+++ b/solution.py
@@ -25,8 +25,9 @@
             send_sem=self.send.at[k, n], recv_sem=self.recv.at[k, n],
             device_id=self.dev(target), device_id_type=MESH)
 
-    def start_own(self, k, src=None):
-        for n, half, target in ((0, 0, self.right), (3, 1, self.left), (1, 1, self.right), (4, 0, self.left)):
+    def start_own(self, k, src=None, order=(0, 3, 1, 4)):
+        for n in order:
+            half, target = ((0, self.right), (1, self.right), None, (1, self.left), (0, self.left))[n]
             self.copy(k, n, self.me, half, target, None if src is None else src(k, half)).start()
 
     def forward(self, k):
@@ -126,11 +127,14 @@
     gain_own = local(gains, gain_buf.at[hid], 4)
     gain_own.start()
 
-    x_ring = Ring(chip, dev_x, lambda k, c, h: xg.at[2 * c + h, k * nc:(k + 1) * nc, :], xr_s, xr_r)
+    x_ring = Ring(chip, dev_x, lambda k, c, h: xg.at[2 * c + (core if h == 0 else 1 - core), k * nc:(k + 1) * nc, :],
+                  xr_s, xr_r)
+    for k in range(N_CHUNK):
+        x_ring.start_own(k, lambda k, h: x_chunk(k, core), order=(0, 4))
+        xd(k, mate, core).wait_recv()
+        x_ring.start_own(k, order=(3, 1))
     for k in range(N_CHUNK):
         x_own[k].wait()
-        xd(k, mate, core).wait_recv()
-        x_ring.start_own(k)
 
     mats = (w_gate, w_up)
 
@@ -173,8 +177,11 @@
 
     wq_in = local(w_qkv.at[:, ds(chip * qb, qb)], q_stage.at[0:width, 0:qb], 8)
     wq_in.start()
-    for n, c in enumerate((right, left, far)):
-        remote(w_qkv.at[:, ds(c * qb, qb)], wq_all.at[row, core, chip], wq_s.at[n], wq_r.at[n], dev_x(c)).start()
+    via, back = lax.rem(chip + 1 + 2 * core, 4), lax.rem(chip + 3 - 2 * core, 4)
+    wq_tmp = q_stage.at[0:width, qb:2 * qb]
+
+    def wq_copy(n, src, owner, c):
+        return remote(src, wq_tmp if n == 2 else wq_all.at[row, core, owner], wq_s.at[n], wq_r.at[n], dev_x(c))
 
     n_ring = Ring(row, dev_y, lambda k, r, h: n_all.at[r, k * nc + h * (nc // 2):k * nc + (h + 1) * (nc // 2), :],
                   nr_s, nr_r)
@@ -221,6 +228,9 @@
         remote(stage.at[0, m], half_rows(m, 2 * left + core, 0), wx_s.at[4, m], wx_r.at[4, m], dev_x(right)).start()
         remote(stage.at[1, m], stage.at[1, m], wx_s.at[1, m], wx_r.at[1, m], dev_x(left)).wait_recv()
         remote(stage.at[1, m], half_rows(m, 2 * right + core, 1), wx_s.at[5, m], wx_r.at[5, m], dev_x(left)).start()
+    wq_copy(2, w_qkv.at[:, ds(far * qb, qb)], chip, via).start()
+    wq_copy(0, w_qkv.at[:, ds(right * qb, qb)], chip, right).start()
+    wq_copy(1, w_qkv.at[:, ds(left * qb, qb)], chip, left).start()
     n_ring.forward(1)
     n_ring.forward(2)
     for m in range(2):
@@ -235,8 +245,6 @@
         remote(stage.at[1, m], half_rows(m, h, 1), wx_s.at[5, m], wx_r.at[5, m], dev_x(left)).wait_recv()
         w_mate(3, m, h).start()
     wq_keep.wait()
-    for n, c in enumerate((left, right, far)):
-        remote(w_qkv.at[:, ds(c * qb, qb)], wq_all.at[row, core, c], wq_s.at[n], wq_r.at[n], dev_x(c)).wait_recv()
     wq_ring = Ring(row, dev_y, lambda k, r, h: wq_all.at[r, core, 2 * h:2 * h + 2], wr_s, wr_r)
     for c in w_own:
         c.wait()
@@ -256,7 +264,7 @@
         r = lax.rem(row + lax.div(s, 2) + 1, 4)
         return local(n_all.at[r, ds(lax.rem(s, 2) * sub, sub), :], n_in, 13)
 
-    def part_copy(s, back):
+    def part_copy(s):
         d = lax.div(s, 2) + 1
         to = lax.rem(row + d, 4)
         return remote(part.at[s], got.at[s], rs_s.at[s], rs_r.at[s], dev_y(to))
@@ -265,64 +273,13 @@
         n_ring.wait_right(k)
     n_load(0).start()
 
-    def step(s, carry):
-        @pl.when(s < 8)
-        def _():
-            n_load(s).wait()
-            gate = jnp.dot(n_in[...], w_in[:, 0:ff], preferred_element_type=jnp.float32).astype(jnp.bfloat16)
-            up = jnp.dot(n_in[...], w_in[:, ff:2 * ff], preferred_element_type=jnp.float32).astype(jnp.bfloat16)
-            act[s, :, ds(chip * ff, ff)] = (
-                jax.nn.silu(gate.astype(jnp.float32)) * up.astype(jnp.float32)).astype(act.dtype)
-            a_ring.start_own(s)
-
-        @pl.when((s >= 1) & (s < 9))
-        def _():
-            a_ring.forward(s - 1)
-
-        @pl.when(s == 1)
-        def _():
-            for k in range(N_CHUNK):
-                n_ring.wait_far(k)
-
-        @pl.when(s == 3)
-        def _():
-            for k in range(N_CHUNK):
-                n_ring.wait_left(k)
-            wq_ring.start_own(0)
-
-        @pl.when(s == 6)
-        def _():
-            wq_ring.forward(0)
-
-        @pl.when(s < 7)
-        def _():
-            n_load(s + 1).start()
-
-        @pl.when(s >= 2)
-        def _():
-            b = s - 2
-            a_ring.finish(b)
-            for c in range(2):
-                part[b, c] = jnp.dot(act[b], wd_in[c], preferred_element_type=jnp.float32).astype(part.dtype)
-
-            @pl.when(b < 6)
-            def _():
-                part_copy(b, 0).start()
-
-        return carry
-
-    lax.fori_loop(0, 10, step, 0)
-
-    wq_ring.finish(0)
-    for r in range(4):
-        remote(wq_all.at[r, core], wq_all.at[r, core], wqd_s.at[r], wqd_r.at[r], mate_dev).start()
-
-    for s in range(6):
-        part_copy(s, 0).wait_recv()
-    for k in range(N_CHUNK):
-        n_ring.drain(k)
-    tile = min(16, sub)
-    for s in range(2):
+    x2_ring = Ring(chip, dev_x, lambda k, c, h: xg.at[2 * c + h, k * qc:(k + 1) * qc, :], x2r_s, x2r_r)
+
+    def add_residual(s):
+        tile = min(16, sub)
+        for q in range(3):
+            part_copy(2 * q + s).wait_recv()
+
         def add(t, carry):
             rows = ds(t * tile, tile)
             out_rows = ds(s * sub + t * tile, tile)
@@ -337,9 +294,87 @@
 
         lax.fori_loop(0, sub // tile, add, 0)
 
-    x2_ring = Ring(chip, dev_x, lambda k, c, h: xg.at[2 * c + h, k * qc:(k + 1) * qc, :], x2r_s, x2r_r)
-    for k in range(Q_CHUNK):
-        x2_ring.start_own(k)
+    def wq_mate(r, c):
+        return remote(wq_all.at[r, c], wq_all.at[r, c], wqd_s.at[r], wqd_r.at[r], mate_dev)
+
+    wq_loads = [local(wq_all.at[r, c, i], w_in.at[(2 * i + c) * width:(2 * i + c + 1) * width, r * qb:(r + 1) * qb],
+                      16 + r * 8 + c * 4 + i) for r in range(4) for c in range(2) for i in range(4)]
+
+    def step(s, carry):
+        @pl.when(s < 8)
+        def _():
+            n_load(s).wait()
+            gate = jnp.dot(n_in[...], w_in[:, 0:ff], preferred_element_type=jnp.float32).astype(jnp.bfloat16)
+            up = jnp.dot(n_in[...], w_in[:, ff:2 * ff], preferred_element_type=jnp.float32).astype(jnp.bfloat16)
+            act[s, :, ds(chip * ff, ff)] = (
+                jax.nn.silu(gate.astype(jnp.float32)) * up.astype(jnp.float32)).astype(act.dtype)
+            a_ring.start_own(s)
+
+        @pl.when((s >= 1) & (s < 9))
+        def _():
+            a_ring.forward(s - 1)
+
+        @pl.when(s == 1)
+        def _():
+            wq_copy(2, w_qkv.at[:, ds(far * qb, qb)], chip, via).wait_recv()
+            wq_copy(3, wq_tmp, back, via).start()
+            for k in range(N_CHUNK):
+                n_ring.wait_far(k)
+
+        @pl.when(s == 3)
+        def _():
+            for k in range(N_CHUNK):
+                n_ring.wait_left(k)
+            for n, c in ((0, left), (1, right), (3, far)):
+                wq_copy(n, wq_tmp, c, c).wait_recv()
+            wq_ring.start_own(0)
+
+        @pl.when(s == 6)
+        def _():
+            wq_ring.forward(0)
+
+        @pl.when(s < 7)
+        def _():
+            n_load(s + 1).start()
+
+        @pl.when(s == 8)
+        def _():
+            wq_ring.finish(0)
+            for r in range(4):
+                wq_mate(r, core).start()
+
+        @pl.when(s >= 2)
+        def _():
+            b = s - 2
+            a_ring.finish(b)
+            for c in range(2):
+                part[b, c] = jnp.dot(act[b], wd_in[c], preferred_element_type=jnp.float32).astype(part.dtype)
+
+            @pl.when(b < 6)
+            def _():
+                part_copy(b).start()
+
+        @pl.when(s == 8)
+        def _():
+            add_residual(0)
+            x2_ring.start_own(0)
+            for m in range(2):
+                for n in range(4):
+                    w_mate(n, m, hid).wait_send()
+            for r in range(4):
+                wq_mate(r, 1 - core).wait_recv()
+            for c in wq_loads:
+                c.start()
+
+        @pl.when(s == 9)
+        def _():
+            x2_ring.forward(0)
+            add_residual(1)
+            x2_ring.start_own(1)
+
+        return carry
+
+    lax.fori_loop(0, 10, step, 0)
 
     def x2_rows(c, r):
         return x2_out.at[ds(rows_of(c, r), block), :]
@@ -348,27 +383,10 @@
     x2_keep.start()
     x2_mate = remote(xg.at[mate], x2_rows(core, row), one_s.at[1], one_r.at[1], mate_dev)
     x2_mate.start()
-
-    for r in range(4):
-        remote(wq_all.at[r, 1 - core], wq_all.at[r, 1 - core], wqd_s.at[r], wqd_r.at[r], mate_dev).wait_recv()
-
-    def wq_load(r, c, i):
-        return local(wq_all.at[r, c, i], w_in.at[(2 * i + c) * width:(2 * i + c + 1) * width, r * qb:(r + 1) * qb],
-                     16 + r * 8 + c * 4 + i)
-
-    wq_loads = [wq_load(r, c, i) for r in range(4) for c in range(2) for i in range(4)]
-    for m in range(2):
-        for n in range(4):
-            w_mate(n, m, hid).wait_send()
-    for c in wq_loads:
-        c.start()
-
-    for k in range(Q_CHUNK):
-        x2_ring.forward(k)
-    x2_keep.wait()
-    remote(xg.at[mate], x2_rows(1 - core, row), one_s.at[1], one_r.at[1], mate_dev).wait_recv()
     out_ring = Ring(row, dev_y, lambda k, r, h: x2_rows(h, r), or_s, or_r)
-    out_ring.start_own(0)
+    for k in range(N_CHUNK):
+        n_ring.drain(k)
+    wq_copy(3, wq_tmp, back, via).wait_send()
     for c in wq_loads:
         c.wait()
 
@@ -387,43 +405,69 @@
 
     q_keep = [local(q_stage.at[k * qc:(k + 1) * qc, ds(row * qb, qb)],
                     qkv_out.at[q_rows(row, k * qc, qc), ds(chip * qb, qb)], 1 + k) for k in range(Q_CHUNK)]
-    for k in range(Q_CHUNK):
-        x2_ring.finish(k)
+    qh = qc // 2
+
+    q_ring = Ring(chip, dev_x,
+                  lambda j, c, h: qkv_out.at[q_rows(lax.rem(row + 4 - j // 2, 4), (j % 2) * qc + h * qh, qh),
+                                             ds(c * qb, qb)],
+                  qr_s, qr_r)
+
+    def q_mate(j, c):
+        rows = ds(rows_of(c, lax.rem(row + 4 - j // 2, 4)) + (j % 2) * qc, qc)
+        return remote(qkv_out.at[rows, :], qkv_out.at[rows, :], qd_s.at[j], qd_r.at[j], mate_dev)
+
+    def qkv(k):
         norm(k * qc, qc, 1)
         q_stage[k * qc:(k + 1) * qc, :] = jnp.dot(
             n_own[k * qc:(k + 1) * qc, :], w_in[:, 0:4 * qb], preferred_element_type=jnp.float32).astype(q_stage.dtype)
-        for n in range(3):
+        for n in (1, 0, 2):
             qy(k, n, lax.rem(row + n + 1, 4)).start()
         q_keep[k].start()
+        q_ring.start_own(k, lambda j, h: q_stage.at[k * qc + h * qh:k * qc + (h + 1) * qh, ds(row * qb, qb)])
+
+    def q_next(n, k):
+        qy_got(k, n - 1, lax.rem(row + 4 - n, 4)).wait_recv()
+        q_ring.start_own(2 * n + k)
+
+    def q_done(n, k):
+        q_ring.finish(2 * n + k)
+        q_mate(2 * n + k, core).start()
+
+    x2_ring.forward(1)
+    x2_ring.finish(0)
+    qkv(0)
+    x2_ring.finish(1)
+    q_ring.forward(0)
+    for n in (1, 3):
+        q_next(n, 0)
+    qkv(1)
+    x2_keep.wait()
+    remote(xg.at[mate], x2_rows(1 - core, row), one_s.at[1], one_r.at[1], mate_dev).wait_recv()
+    out_ring.start_own(0)
+    q_next(2, 0)
+    for n in (1, 3):
+        q_ring.forward(2 * n)
+    q_ring.forward(1)
+    q_keep[0].wait()
+    q_done(0, 0)
+    q_next(1, 1)
+    q_ring.forward(4)
+    q_done(1, 0)
+    q_next(3, 1)
+    q_ring.forward(3)
+    q_done(3, 0)
+    q_next(2, 1)
+    q_ring.forward(7)
+    q_keep[1].wait()
+    q_done(0, 1)
+    q_done(2, 0)
     out_ring.forward(0)
-
-    q_ring = Ring(chip, dev_x,
-                  lambda n, c, h: qkv_out.at[ds(rows_of(core, lax.rem(row + 4 - n, 4)) + h * sub, sub), ds(c * qb, qb)],
-                  qr_s, qr_r)
-
-    def q_mate(n, c):
-        rows = ds(rows_of(c, lax.rem(row + 4 - n, 4)), block)
-        return remote(qkv_out.at[rows, :], qkv_out.at[rows, :], qd_s.at[n], qd_r.at[n], mate_dev)
-
-    for c in q_keep:
-        c.wait()
-    q_ring.start_own(0)
-    for n in range(1, 4):
-        for k in range(Q_CHUNK):
-            qy_got(k, n - 1, lax.rem(row + 4 - n, 4)).wait_recv()
-        q_ring.start_own(n)
-        q_ring.forward(n - 1)
-        if n >= 2:
-            q_ring.finish(n - 2)
-            q_mate(n - 2, core).start()
-    q_ring.forward(3)
-    for n in (2, 3):
-        q_ring.finish(n)
-        q_mate(n, core).start()
+    q_ring.forward(5)
+    q_done(1, 1)
+    q_done(3, 1)
+    q_done(2, 1)
     out_ring.finish(0)
 
-    for n in range(4):
-        q_mate(n, 1 - core).wait_recv()
     for d in range(1, 8):
         gain_copy(d).wait_send()
     for k in range(N_CHUNK):
@@ -432,23 +476,21 @@
     x2_mate.wait_send()
     for m in range(2):
         for n in range(6):
-            remote(stage.at[0, m] if n in (0, 1, 4, 5) else w_rows(m, hid),
-                   stage.at[0, m] if n in (0, 1, 4, 5) else w_rows(m, hid),
-                   wx_s.at[n, m], wx_r.at[n, m], dev_x(right)).wait_send()
+            ref = stage.at[0, m] if n in (0, 1, 4, 5) else w_rows(m, hid)
+            remote(ref, ref, wx_s.at[n, m], wx_r.at[n, m], dev_x(right)).wait_send()
     for n in range(3):
-        remote(wq_all.at[row, core, chip], wq_all.at[row, core, chip], wq_s.at[n], wq_r.at[n],
-               dev_x(right)).wait_send()
+        wq_copy(n, wq_tmp, chip, right).wait_send()
     for r in range(4):
-        remote(wq_all.at[r, core], wq_all.at[r, core], wqd_s.at[r], wqd_r.at[r], mate_dev).wait_send()
+        wq_mate(r, core).wait_send()
     for s in range(6):
-        part_copy(s, 0).wait_send()
+        part_copy(s).wait_send()
     for k in range(Q_CHUNK):
         for n in range(3):
             qy(k, n, lax.rem(row + n + 1, 4)).wait_send()
         x2_ring.drain(k)
-    for n in range(4):
-        q_mate(n, core).wait_send()
-        q_ring.drain(n)
+    for j in range(4 * Q_CHUNK):
+        q_mate(j, core).wait_send()
+        q_ring.drain(j)
 
     def drain_act(s, carry):
         a_ring.drain(s)
@@ -457,6 +499,8 @@
     lax.fori_loop(0, 8, drain_act, 0)
     wq_ring.drain(0)
     out_ring.drain(0)
+    for j in range(4 * Q_CHUNK):
+        q_mate(j, 1 - core).wait_recv()
 
 
 def solution(mesh):
@@ -494,11 +538,11 @@
                 pltpu.VMEM((8, 2, width), jnp.float32),
                 dma((48,)), dma((2,)), dma((2,)), dma((7,)), dma((7,)),
                 dma((N_CHUNK,)), dma((N_CHUNK,)), dma((6, 2)), dma((6, 2)), dma((4, 2)), dma((4, 2)),
-                dma((3,)), dma((3,)), dma((4,)), dma((4,)), dma((6,)), dma((6,)),
-                dma((Q_CHUNK, 3)), dma((Q_CHUNK, 3)), dma((4,)), dma((4,)),
+                dma((4,)), dma((4,)), dma((4,)), dma((4,)), dma((6,)), dma((6,)),
+                dma((Q_CHUNK, 3)), dma((Q_CHUNK, 3)), dma((4 * Q_CHUNK,)), dma((4 * Q_CHUNK,)),
                 dma((N_CHUNK, 6)), dma((N_CHUNK, 6)), dma((N_CHUNK, 6)), dma((N_CHUNK, 6)),
                 dma((8, 6)), dma((8, 6)), dma((1, 6)), dma((1, 6)), dma((Q_CHUNK, 6)), dma((Q_CHUNK, 6)),
-                dma((1, 6)), dma((1, 6)), dma((4, 6)), dma((4, 6)),
+                dma((1, 6)), dma((1, 6)), dma((4 * Q_CHUNK, 6)), dma((4 * Q_CHUNK, 6)),
             ],
             compiler_params=pltpu.CompilerParams(
                 collective_id=0, has_side_effects=True, vmem_limit_bytes=67043328),

time: 412 us -> 392 us (0.951)
  Pallas kernels: 395 us -> 375 us
    pallas_call x1, Pallas kernels: 395 us -> 375 us  [device_step(): pl.pallas_call(functools.partial(kernel, d_model), out_shape=(jax.ShapeDt...]
where the time goes in v2:
time: 392 us
  Pallas kernels  375 us (96%)
  local copies, waits for them, and re-layouts  14.9 us (4%)
    pallas_call x1, Pallas kernels, device_step(): pl.pallas_call(functools.partial(kernel, d_model), out_shape=(jax.ShapeDt...  375 us
    unnamed x2, local copies, waits for them, and re-layouts  14.9 us

profile of v2, /device:TPU:97, one launch (start us, length us, event | category | flops | bytes accessed | tf_op | source)
XLA Modules:
  0.0 391.5 jit_solution(3454082481952234862)
XLA Ops:
  0.6 1.3 pad_maximum_fusion.gains
  1.9 374.6 %layer.1 = (bf16[4096,512]{1,0:T(8,128)(2,1)}, bf16[4096,1536]{1,0:T(8,128)(2,1)}, bf16[4,512,4096]{2,1,0:T(8,128)(2,1)}, bf16[4,2,4,512,384]{4,3,2,1,0:T(8,128)(2,1)}) custom-call(bf16[4096,512]{1,0:T(8,128)(2,1)} %x.1, f32[2,512]{1,0:T(2,128)} %pad_maximum_fusion.gains, bf16[512,3584]{1,0:T(8,128)(2,1)} %w_gate.1, bf16[512,3584]{1,0:T(8,128)(2,1)} %w_up.1, ...), custom_call_target="tpu_custom_call" | custom-call | tf_op jit(solution)/shard_map/layer/pallas_call | solution.py:519
  376.6 4.5 %copy.11 = bf16[4096,512]{1,0:T(8,128)(2,1)} copy(bf16[4096,512]{1,0:T(8,128)(2,1)} %get-tuple-element.8) | data formatting | bytes 8388608
  381.1 10.5 %copy.12 = bf16[4096,1536]{1,0:T(8,128)(2,1)} copy(bf16[4096,1536]{1,0:T(8,128)(2,1)} %get-tuple-element.9) | data formatting | bytes 25165824

commit v3 on v2

--- a/solution.py
+++ b/solution.py
@@ -58,7 +58,7 @@
             self.copy(k, n, owner, half, target).wait_send()
 
 
-def kernel(d_model, x, gains, w_gate, w_up, w_down, w_qkv,
+def kernel(d_model, x, gain_a, gain_b, w_gate, w_up, w_down, w_qkv,
            x2_out, qkv_out, n_all, wq_all,
            xg, n_own, n_in, w_in, stage, act, wd_in, part, got, q_stage, gain_buf,
            loc, one_s, one_r, gain_s, gain_r, xd_s, xd_r, wx_s, wx_r, wd_s, wd_r, wq_s, wq_r, wqd_s, wqd_r,
@@ -114,18 +114,17 @@
         xd(k, hid, 1 - core).start()
         x_own[k].start()
 
-    def gain_copy(d):
+    gains = (gain_a, gain_b)
+
+    def gain_copy(d, m):
         to = lax.rem(hid + d, 8)
-        return remote(gains, gain_buf.at[hid], gain_s.at[d - 1], gain_r.at[d - 1], {'hid': to, 'ffn': row})
-
-    def gain_got(d):
+        return remote(gains[m], gain_buf.at[m, hid], gain_s.at[d - 1, m], gain_r.at[d - 1, m], {'hid': to, 'ffn': row})
+
+    def gain_got(d, m):
         src = lax.rem(hid + 8 - d, 8)
-        return remote(gains, gain_buf.at[src], gain_s.at[d - 1], gain_r.at[d - 1], {'hid': src, 'ffn': row})
-
-    for d in range(1, 8):
-        gain_copy(d).start()
-    gain_own = local(gains, gain_buf.at[hid], 4)
-    gain_own.start()
+        return remote(gains[m], gain_buf.at[m, src], gain_s.at[d - 1, m], gain_r.at[d - 1, m], {'hid': src, 'ffn': row})
+
+    gain_own = [local(gains[m], gain_buf.at[m, hid], (4, 15)[m]) for m in range(2)]
 
     x_ring = Ring(chip, dev_x, lambda k, c, h: xg.at[2 * c + (core if h == 0 else 1 - core), k * nc:(k + 1) * nc, :],
                   xr_s, xr_r)
@@ -133,6 +132,10 @@
         x_ring.start_own(k, lambda k, h: x_chunk(k, core), order=(0, 4))
         xd(k, mate, core).wait_recv()
         x_ring.start_own(k, order=(3, 1))
+    for m in range(2):
+        gain_own[m].start()
+        for d in range(1, 8):
+            gain_copy(d, m).start()
     for k in range(N_CHUNK):
         x_own[k].wait()
 
@@ -202,14 +205,15 @@
             for h in range(8):
                 piece = xg[h, rows, :].astype(jnp.float32)
                 n_own[rows, h * width:(h + 1) * width] = (
-                    piece * scale * gain_buf[h, which:which + 1, :]).astype(n_own.dtype)
+                    piece * scale * gain_buf[which, h]).astype(n_own.dtype)
             return carry
 
         lax.fori_loop(0, count // tile, body, 0)
 
-    gain_own.wait()
-    for d in range(1, 8):
-        gain_got(d).wait_recv()
+    for m in range(2):
+        gain_own[m].wait()
+        for d in range(1, 8):
+            gain_got(d, m).wait_recv()
     n_keep = [local(n_own.at[k * nc:(k + 1) * nc, :], n_all.at[row, k * nc:(k + 1) * nc, :], 9 + k)
               for k in range(N_CHUNK)]
     for k in range(N_CHUNK):
@@ -257,8 +261,10 @@
         n_keep[k].wait()
         x_ring.drain(k)
 
-    a_ring = Ring(chip, dev_x, lambda s, c, h: act.at[s, h * (sub // 2):(h + 1) * (sub // 2), ds(c * ff, ff)],
-                  ar_s, ar_r)
+    def part_rows(h, start, count):
+        return pl.ds(start + h * (count // 2), count // 2)
+
+    a_ring = Ring(chip, dev_x, lambda s, c, h: act.at[s, part_rows(h, 0, sub), ds(c * ff, ff)], ar_s, ar_r)
 
     def n_load(s):
         r = lax.rem(row + lax.div(s, 2) + 1, 4)
@@ -343,9 +349,9 @@
             for r in range(4):
                 wq_mate(r, core).start()
 
-        @pl.when(s >= 2)
-        def _():
-            b = s - 2
+        @pl.when(s >= 3)
+        def _():
+            b = s - 3
             a_ring.finish(b)
             for c in range(2):
                 part[b, c] = jnp.dot(act[b], wd_in[c], preferred_element_type=jnp.float32).astype(part.dtype)
@@ -354,7 +360,7 @@
             def _():
                 part_copy(b).start()
 
-        @pl.when(s == 8)
+        @pl.when(s == 9)
         def _():
             add_residual(0)
             x2_ring.start_own(0)
@@ -366,7 +372,7 @@
             for c in wq_loads:
                 c.start()
 
-        @pl.when(s == 9)
+        @pl.when(s == 10)
         def _():
             x2_ring.forward(0)
             add_residual(1)
@@ -374,7 +380,7 @@
 
         return carry
 
-    lax.fori_loop(0, 10, step, 0)
+    lax.fori_loop(0, 11, step, 0)
 
     def x2_rows(c, r):
         return x2_out.at[ds(rows_of(c, r), block), :]
@@ -405,10 +411,9 @@
 
     q_keep = [local(q_stage.at[k * qc:(k + 1) * qc, ds(row * qb, qb)],
                     qkv_out.at[q_rows(row, k * qc, qc), ds(chip * qb, qb)], 1 + k) for k in range(Q_CHUNK)]
-    qh = qc // 2
 
     q_ring = Ring(chip, dev_x,
-                  lambda j, c, h: qkv_out.at[q_rows(lax.rem(row + 4 - j // 2, 4), (j % 2) * qc + h * qh, qh),
+                  lambda j, c, h: qkv_out.at[part_rows(h, rows_of(core, lax.rem(row + 4 - j // 2, 4)) + (j % 2) * qc, qc),
                                              ds(c * qb, qb)],
                   qr_s, qr_r)
 
@@ -423,7 +428,7 @@
         for n in (1, 0, 2):
             qy(k, n, lax.rem(row + n + 1, 4)).start()
         q_keep[k].start()
-        q_ring.start_own(k, lambda j, h: q_stage.at[k * qc + h * qh:k * qc + (h + 1) * qh, ds(row * qb, qb)])
+        q_ring.start_own(k, lambda j, h: q_stage.at[part_rows(h, k * qc, qc), ds(row * qb, qb)])
 
     def q_next(n, k):
         qy_got(k, n - 1, lax.rem(row + 4 - n, 4)).wait_recv()
@@ -469,7 +474,8 @@
     out_ring.finish(0)
 
     for d in range(1, 8):
-        gain_copy(d).wait_send()
+        for m in range(2):
+            gain_copy(d, m).wait_send()
     for k in range(N_CHUNK):
         xd(k, hid, 1 - core).wait_send()
     wd_mate.wait_send()
@@ -503,6 +509,37 @@
         q_mate(j, 1 - core).wait_recv()
 
 
+def settle_kernel(pieces, a, b, a_out, b_out, a_buf, b_buf, read, write):
+    copies = []
+    for n, (src, buf, dst) in enumerate(((b, b_buf, b_out), (a, a_buf, a_out))):
+        rows = src.shape[0] // pieces
+        for p in range(pieces):
+            at = pl.ds(p * rows, rows)
+            copies.append((pltpu.make_async_copy(src.at[at, :], buf.at[at, :], read.at[n, p]),
+                           pltpu.make_async_copy(buf.at[at, :], dst.at[at, :], write.at[n, p])))
+    for into, _ in copies:
+        into.start()
+    for into, out in copies:
+        into.wait()
+        out.start()
+    for _, out in copies:
+        out.wait()
+
+
+def settle(a, b):
+    pieces = 8
+    spec = pl.BlockSpec(memory_space=pl.ANY)
+    dma = pltpu.SemaphoreType.DMA
+    return pl.pallas_call(
+        functools.partial(settle_kernel, pieces),
+        out_shape=(jax.ShapeDtypeStruct(a.shape, a.dtype), jax.ShapeDtypeStruct(b.shape, b.dtype)),
+        in_specs=[spec] * 2, out_specs=(spec,) * 2,
+        scratch_shapes=[pltpu.VMEM(a.shape, a.dtype), pltpu.VMEM(b.shape, b.dtype), dma((2, pieces)), dma((2, pieces))],
+        compiler_params=pltpu.CompilerParams(vmem_limit_bytes=67043328),
+        name='settle',
+    )(a, b)
+
+
 def solution(mesh):
     hid_ways, ffn_ways = mesh.shape['hid'], mesh.shape['ffn']
     assert hid_ways == 8 and ffn_ways == 4
@@ -512,7 +549,6 @@
         d_model = width * hid_ways
         block, sub = tokens // 8, tokens // 16
         ff, qb = w_gate.shape[1] // 4, w_qkv.shape[1] // 4
-        gains = jnp.stack([gain_mlp, gain_attn])
         dtype = residual.dtype
         any_spec = pl.BlockSpec(memory_space=pl.ANY)
         dma = pltpu.SemaphoreType.DMA
@@ -522,7 +558,7 @@
                        jax.ShapeDtypeStruct((tokens, w_qkv.shape[1]), dtype),
                        jax.ShapeDtypeStruct((4, block, d_model), dtype),
                        jax.ShapeDtypeStruct((4, 2, 4, width, qb), dtype)),
-            in_specs=[any_spec] * 6,
+            in_specs=[any_spec] * 7,
             out_specs=(any_spec,) * 4,
             scratch_shapes=[
                 pltpu.VMEM((8, block, width), dtype),
@@ -535,8 +571,8 @@
                 pltpu.VMEM((8, 2, sub, width), dtype),
                 pltpu.VMEM((6, 2, sub, width), dtype),
                 pltpu.VMEM((max(block, width), 4 * qb), dtype),
-                pltpu.VMEM((8, 2, width), jnp.float32),
-                dma((48,)), dma((2,)), dma((2,)), dma((7,)), dma((7,)),
+                pltpu.VMEM((2, 8, 1, width), jnp.float32),
+                dma((48,)), dma((2,)), dma((2,)), dma((7, 2)), dma((7, 2)),
                 dma((N_CHUNK,)), dma((N_CHUNK,)), dma((6, 2)), dma((6, 2)), dma((4, 2)), dma((4, 2)),
                 dma((4,)), dma((4,)), dma((4,)), dma((4,)), dma((6,)), dma((6,)),
                 dma((Q_CHUNK, 3)), dma((Q_CHUNK, 3)), dma((4 * Q_CHUNK,)), dma((4 * Q_CHUNK,)),
@@ -547,8 +583,8 @@
             compiler_params=pltpu.CompilerParams(
                 collective_id=0, has_side_effects=True, vmem_limit_bytes=67043328),
             name='layer',
-        )(residual, gains, w_gate, w_up, w_down, w_qkv)
-        return outs[0], outs[1]
+        )(residual, gain_mlp[None, :], gain_attn[None, :], w_gate, w_up, w_down, w_qkv)
+        return settle(outs[0], outs[1])
 
     return jax.shard_map(
         device_step, mesh=mesh,

time: 392 us -> 380 us (0.969)
  local copies, waits for them, and re-layouts: 14.9 us -> 0 us
  Pallas kernels: 375 us -> 379 us
    unnamed x2 -> x0, local copies, waits for them, and re-layouts: 14.9 us -> none
    pallas_call x0 -> x1, Pallas kernels: none -> 12 us  [settle(): pl.pallas_call(functools.partial(settle_kernel, pieces), out_shape=(jax.S...]
    pallas_call x1, Pallas kernels: 375 us -> 367 us  [device_step(): pl.pallas_call(functools.partial(kernel, d_model), out_shape=(jax.ShapeDt...]
where the time goes in v3:
time: 380 us
  Pallas kernels  379 us (100%)
    pallas_call x1, Pallas kernels, device_step(): pl.pallas_call(functools.partial(kernel, d_model), out_shape=(jax.ShapeDt...  367 us
    pallas_call x1, Pallas kernels, settle(): pl.pallas_call(functools.partial(settle_kernel, pieces), out_shape=(jax.S...  12 us

profile of v3, /device:TPU:97, one launch (start us, length us, event | category | flops | bytes accessed | tf_op | source)
XLA Modules:
  0.0 380.1 jit_solution(12924494501593500894)
XLA Ops:
  0.6 367.3 %layer.1 = (bf16[4096,512]{1,0:T(8,128)(2,1)}, bf16[4096,1536]{1,0:T(8,128)(2,1)}, bf16[4,512,4096]{2,1,0:T(8,128)(2,1)}, bf16[4,2,4,512,384]{4,3,2,1,0:T(8,128)(2,1)}) custom-call(bf16[4096,512]{1,0:T(8,128)(2,1)} %x.1, f32[1,512]{1,0:T(1,128)} %bitcast.2, f32[1,512]{1,0:T(1,128)} %bitcast.3, bf16[512,3584]{1,0:T(8,128)(2,1)} %w_gate.1, ...), custom_call_target="tpu_custom_call" | custom-call | tf_op jit(solution)/shard_map/layer/pallas_call | solution.py:555
  367.9 12.0 %settle.1 = (bf16[4096,512]{1,0:T(8,128)(2,1)}, bf16[4096,1536]{1,0:T(8,128)(2,1)}) custom-call(bf16[4096,512]{1,0:T(8,128)(2,1)} %get-tuple-element.4.a, bf16[4096,1536]{1,0:T(8,128)(2,1)} %get-tuple-element.5.b), custom_call_target="tpu_custom_call" | custom-call | tf_op jit(solution)/shard_map/settle/pallas_call | solution.py:533

commit v4 on v3

--- a/solution.py
+++ b/solution.py
@@ -266,13 +266,16 @@
 
     a_ring = Ring(chip, dev_x, lambda s, c, h: act.at[s, part_rows(h, 0, sub), ds(c * ff, ff)], ar_s, ar_r)
 
+    def ahead(s):
+        q = lax.div(s, 2)
+        return lax.rem(2 * q + 1 + lax.div(q, 2), 4)
+
     def n_load(s):
-        r = lax.rem(row + lax.div(s, 2) + 1, 4)
+        r = lax.rem(row + ahead(s), 4)
         return local(n_all.at[r, ds(lax.rem(s, 2) * sub, sub), :], n_in, 13)
 
     def part_copy(s):
-        d = lax.div(s, 2) + 1
-        to = lax.rem(row + d, 4)
+        to = lax.rem(row + ahead(s), 4)
         return remote(part.at[s], got.at[s], rs_s.at[s], rs_r.at[s], dev_y(to))
 
     for k in range(N_CHUNK):
@@ -325,12 +328,12 @@
             wq_copy(2, w_qkv.at[:, ds(far * qb, qb)], chip, via).wait_recv()
             wq_copy(3, wq_tmp, back, via).start()
             for k in range(N_CHUNK):
+                n_ring.wait_left(k)
+
+        @pl.when(s == 3)
+        def _():
+            for k in range(N_CHUNK):
                 n_ring.wait_far(k)
-
-        @pl.when(s == 3)
-        def _():
-            for k in range(N_CHUNK):
-                n_ring.wait_left(k)
             for n, c in ((0, left), (1, right), (3, far)):
                 wq_copy(n, wq_tmp, c, c).wait_recv()
             wq_ring.start_own(0)

time: 380 us -> 365 us (0.961)
  Pallas kernels: 379 us -> 364 us
    pallas_call x1, Pallas kernels: 367 us -> 352 us  [device_step(): pl.pallas_call(functools.partial(kernel, d_model), out_shape=(jax.ShapeDt...]
where the time goes in v4:
time: 365 us
  Pallas kernels  364 us (100%)
    pallas_call x1, Pallas kernels, device_step(): pl.pallas_call(functools.partial(kernel, d_model), out_shape=(jax.ShapeDt...  352 us
    pallas_call x1, Pallas kernels, settle(): pl.pallas_call(functools.partial(settle_kernel, pieces), out_shape=(jax.S...  12 us

profile of v4, /device:TPU:97, one launch (start us, length us, event | category | flops | bytes accessed | tf_op | source)
XLA Modules:
  0.0 364.5 jit_solution(15969516584091274985)
XLA Ops:
  0.6 351.7 %layer.1 = (bf16[4096,512]{1,0:T(8,128)(2,1)}, bf16[4096,1536]{1,0:T(8,128)(2,1)}, bf16[4,512,4096]{2,1,0:T(8,128)(2,1)}, bf16[4,2,4,512,384]{4,3,2,1,0:T(8,128)(2,1)}) custom-call(bf16[4096,512]{1,0:T(8,128)(2,1)} %x.1, f32[1,512]{1,0:T(1,128)} %bitcast.2, f32[1,512]{1,0:T(1,128)} %bitcast.3, bf16[512,3584]{1,0:T(8,128)(2,1)} %w_gate.1, ...), custom_call_target="tpu_custom_call" | custom-call | tf_op jit(solution)/shard_map/layer/pallas_call | solution.py:558
  352.3 12.0 %settle.1 = (bf16[4096,512]{1,0:T(8,128)(2,1)}, bf16[4096,1536]{1,0:T(8,128)(2,1)}) custom-call(bf16[4096,512]{1,0:T(8,128)(2,1)} %get-tuple-element.4.a, bf16[4096,1536]{1,0:T(8,128)(2,1)} %get-tuple-element.5.b), custom_call_target="tpu_custom_call" | custom-call | tf_op jit(solution)/shard_map/settle/pallas_call | solution.py:536
